TPU v7x, 32 devices: a whole 2x2x4 slice. The times are simulated.
32 devices in a mesh: batch: 4 (over z), seq: 8 (over y, x, core).
Axes of the slice: x: 2, y: 2, z: 4, core: 2. Of those that a mesh axis runs over, the one named last changes fastest.
Arguments:
- hidden: bfloat16 [4, 4096, 4096], P('batch', 'seq'), may hold values from -6 to 6
- score_direction: bfloat16 [4, 4096, 4096], P('batch', 'seq'), may hold values from -6 to 6
- adapter_down: bfloat16 [4096, 256], replicated, may hold values from -0.09375 to 0.09375
- adapter_up: bfloat16 [4096, 256], replicated, may hold values from -0.09375 to 0.09375
- rewards: float32 [4, 4096], P('batch', 'seq'), may hold values from -0.3125 to 0.3125
- values: float32 [4, 4096], P('batch', 'seq'), may hold values from -120 to 120
- log_ratio: float32 [4, 4096], P('batch', 'seq'), may hold values from -4 to 4
- lengths: int32 [4], P('batch'), may hold values from 1024 to 4096
Outputs:
- returns: float32 [4, 4096], P('batch', 'seq')
- grad_down: float32 [4096, 256], P(('batch', 'seq'))
- grad_up: float32 [4096, 256], P(('batch', 'seq'))
All inputs are finite; a program needn't handle non-finite values.
Results may differ from a plain program's by a relative error of at most 0.0029.
Values sent between devices are 32-bit elements; how exact they have to be, the bound alone decides.
No kernel may reach another device: no remote copies, remote signals or barrier semaphores. Data moves between devices by JAX's collectives and lax.ppermute only.
A program may use at most 128 MiB of HBM per device.

v0:
```python
import math
import jax
import jax.numpy as jnp
from jax import lax
from jax.sharding import PartitionSpec as P

ratio_cap = 2.0
weight_gain = 0.08


def local(hidden, score_direction, adapter_down, adapter_up, rewards, values, log_ratio, lengths):
    seq_count, shard_len, model_width = hidden.shape
    low_rank_product = adapter_down.shape[1]
    shard_total = lax.axis_size("seq")
    total_len = shard_len * shard_total
    seq_total = seq_count * lax.axis_size("batch")
    shard_id = lax.axis_index("seq")
    inner = jnp.arange(shard_len, dtype=jnp.int32)
    positions = shard_id * shard_len + inner
    valid = (positions[None, :] < lengths[:, None]).astype(jnp.float32)
    adapter_scale = 1.0 / math.sqrt(low_rank_product)
    down_projected = jnp.einsum(
        "ogz,zw->ogw", hidden, adapter_down, preferred_element_type=jnp.float32
    )
    up_projected = jnp.einsum(
        "ogz,zw->ogw", score_direction, adapter_up, preferred_element_type=jnp.float32
    )
    weight_update = adapter_scale * jnp.sum(down_projected * up_projected, axis=-1)
    importance = jnp.exp(log_ratio + weight_update)
    live = rewards * valid
    offsets = (inner[None, :] - inner[:, None]).astype(jnp.float32)
    discount_mat = jnp.where(offsets >= 0, jnp.exp(-offsets / total_len), jnp.zeros_like(offsets))
    within = jnp.einsum("sk,tk->st", live, discount_mat, precision=lax.Precision.HIGHEST)
    firsts = within[:, 0]
    every_first = lax.all_gather(firsts[:, None], "seq", axis=1, tiled=True)
    blocks = jnp.arange(shard_total, dtype=jnp.int32)
    steps_back = (blocks - shard_id - 1).astype(jnp.float32)
    weights_blk = jnp.where(
        blocks > shard_id, jnp.exp(-steps_back * shard_len / total_len), jnp.zeros_like(steps_back)
    )
    carried = jnp.sum(every_first * weights_blk[None, :], axis=1)
    tail_decay = jnp.exp(-(shard_len - inner).astype(jnp.float32) / total_len)
    returns = within + tail_decay[None, :] * carried[:, None]
    advantage = returns - values
    seq_weight = (
        weight_gain
        * math.sqrt(total_len * low_rank_product / seq_total)
        / lengths.astype(jnp.float32)
    )
    token_weights = valid * jnp.minimum(importance, ratio_cap) * advantage * seq_weight[:, None]
    up_scaled_map = (-adapter_scale * token_weights[:, :, None] * up_projected).astype(jnp.bfloat16)
    down_scaled_map = (-adapter_scale * token_weights[:, :, None] * down_projected).astype(
        jnp.bfloat16
    )
    group_total = lax.axis_size(("batch", "seq"))
    own_rows = model_width // group_total
    clip_norm = 0.5 * math.sqrt(2.0 * model_width * low_rank_product)
    partial_terms = jnp.concatenate(
        [
            jnp.einsum("oxe,oxq->eq", hidden, up_scaled_map, preferred_element_type=jnp.float32),
            jnp.einsum(
                "oxe,oxq->eq", score_direction, down_scaled_map, preferred_element_type=jnp.float32
            ),
        ],
        axis=1,
    )
    summed = lax.psum(partial_terms, ("batch", "seq"))
    squares = jnp.sum(summed * summed)
    own_part = lax.dynamic_slice_in_dim(
        summed, lax.axis_index(("batch", "seq")) * own_rows, own_rows, 0
    )
    grad_norm = jnp.sqrt(squares)
    factor = clip_norm / jnp.maximum(grad_norm, clip_norm)
    return (
        returns,
        own_part[:, :low_rank_product] * factor,
        own_part[:, low_rank_product:] * factor,
    )


def solution(mesh):
    placed = (
        P("batch", "seq", None),
        P("batch", "seq", None),
        P(),
        P(),
        P("batch", "seq"),
        P("batch", "seq"),
        P("batch", "seq"),
        P("batch"),
    )
    return jax.shard_map(
        local,
        mesh=mesh,
        in_specs=placed,
        out_specs=(P("batch", "seq"), P(("batch", "seq"), None), P(("batch", "seq"), None)),
        check_vma=False,
    )
```

profile of v0, /device:TPU:0, one launch (start us, length us, event | category | flops | bytes accessed | tf_op | source)
XLA Modules:
  0.0 237.2 jit_solution(16906972712396040121)
XLA Ops:
  7.2 0.0 copy-start
  7.2 0.0 all-reduce.3.cloned.1.call-start
  8.0 1.8 fusion.6
  9.9 0.5 slice.12
  10.4 1.2 dynamic-slice
  11.6 1.3 bitcast_dynamic-update-slice_fusion
  13.0 15.2 %all-reduce = f32[8]{0:T(128)S(1)} all-reduce(f32[8]{0:T(128)S(1)} %bitcast_dynamic-update-slice_fusion), channel_id=1, replica_groups=mesh['batch'=4,'seq'=8] {'seq'}, use_global_device_ids=true, to_apply=%add | all-reduce | flops 8 | bytes 64
  28.1 0.6 fusion.26
  28.7 0.0 copy-start.1
  28.7 4.3 %fusion.1 = f32[512,256]{0,1:T(8,128)S(1)} fusion(bf16[4096,256]{1,0:T(8,128)(2,1)} %param.11, bf16[1,512,4096]{2,1,0:T(8,128)(2,1)} %param.9), kind=kOutput, calls=%fused_computation.5 | convolution fusion | flops 1073741824 | bytes 6815744 | tf_op jit(solution)/shard_map/ogz,zw->ogw/dot_general | solution.py:25
  33.0 0.0 copy-done
  33.0 0.0 copy-done.1
  33.1 0.0 copy-start.4
  33.1 0.0 copy-start.5
  33.1 1.3 multiply_reduce_fusion.1
  34.5 0.7 multiply_add_fusion
  35.1 0.0 copy-start.3
  35.1 0.0 copy-done.4
  35.2 0.0 copy-done.5
  35.2 0.0 copy-start.2
  35.2 1.3 convolution_bitcast_fusion.1
  36.5 0.0 copy-done.3
  36.5 0.9 copy-done.2
  37.4 1.3 convolution_bitcast_fusion
  38.7 3.8 %pad_maximum_fusion = f32[4096,512]{0,1:T(8,128)} fusion(f32[4096,256]{0,1:T(8,128)S(1)} %convolution_bitcast_fusion, f32[4096,256]{0,1:T(8,128)S(1)} %convolution_bitcast_fusion.1), kind=kLoop, calls=%fused_computation | loop fusion | flops 2097152 | bytes 16777216 | tf_op jit(solution)/shard_map/concatenate | solution.py:58
  42.4 0.0 all-reduce.3.cloned.1.call-update
  42.4 178.5 %all-reduce.3.cloned.1.call-done = f32[4096,512]{0,1:T(8,128)} async-done(((f32[4096,512]{0,1:T(8,128)}), f32[4096,512]{0,1:T(8,128)}) %all-reduce.3.cloned.1.call-update) | async-done | bytes 8388624 | tf_op jit(solution)/shard_map/psum | solution.py:67
  220.9 6.1 %multiply_reduce_fusion = f32[]{:T(128)} fusion(f32[4096,512]{0,1:T(8,128)} %all-reduce.3.cloned.1.call-done), kind=kLoop, calls=%fused_computation.1 | loop fusion | flops 4194303 | bytes 8388612 | tf_op jit(solution)/shard_map/reduce_sum | solution.py:68
  227.8 1.0 dynamic-slice_multiply_fusion
  228.8 0.8 copy.12
  229.6 0.8 copy.11
  (3 shorter events, 0.0 us)
Async XLA Ops:
  7.2 25.9 %copy-start = (bf16[4096,256]{1,0:T(8,128)(2,1)S(1)}, bf16[4096,256]{1,0:T(8,128)(2,1)}, u32[]{:S(2)}) copy-start(bf16[4096,256]{1,0:T(8,128)(2,1)} %param.10) | copy-start | bytes 6291460
  7.2 213.7 %all-reduce.3.cloned.1.call-start = ((), (), s32[]{:S(2)}) async-start(), calls=%async_computation | async-start | bytes 16777216 | tf_op jit(solution)/shard_map/psum | solution.py:67
  28.7 4.3 %copy-start.1 = (bf16[1,512,4096]{2,1,0:T(8,128)(2,1)S(1)}, bf16[1,512,4096]{2,1,0:T(8,128)(2,1)}, u32[]{:S(2)}) copy-start(bf16[1,512,4096]{2,1,0:T(8,128)(2,1)} %param.8) | copy-start | bytes 12582916
  33.1 2.1 copy-start.4
  33.1 2.1 copy-start.5
  35.1 1.4 copy-start.3
  35.2 2.2 copy-start.2
Sparse Core Ops, SparseCore 0:
  42.6 178.3 all-reduce.2
where the time goes:
time: 237 us
  waiting for transfers between devices  178 us (75%)
  between operations  15.7 us (7%)
  blocking collectives  15.2 us (6%)
  other arithmetic  12.2 us (5%)
  matrix products  10 us (4%)
  local copies, waits for them, and re-layouts  5.52 us (2%)
    psum x1, waiting for transfers between devices, local(): summed = lax.psum(partial_terms, ('batch', 'seq'))  178 us
    unnamed x1, blocking collectives  15.2 us
    reduce_sum x1, other arithmetic, local(): squares = jnp.sum(summed * summed)  6.14 us
    unnamed x17, local copies, waits for them, and re-layouts  5 us
  transfers between devices with their start and end apart: 1, of which 1 were waited for; matrix products, arithmetic and copies ran while one was open for 0% of the time, Pallas kernels for 0%

commit v1 on v0

--- a/solution.py
+++ b/solution.py
@@ -64,7 +64,7 @@
         ],
         axis=1,
     )
-    summed = lax.psum(partial_terms, ("batch", "seq"))
+    summed = lax.psum(lax.psum(partial_terms, "seq"), "batch")
     squares = jnp.sum(summed * summed)
     own_part = lax.dynamic_slice_in_dim(
         summed, lax.axis_index(("batch", "seq")) * own_rows, own_rows, 0

time: 237 us -> 478 us (2.02)
  waiting for transfers between devices: 178 us -> 419 us
    psum x1 -> x2, waiting for transfers between devices: 178 us -> 419 us  [local(): summed = lax.psum(lax.psum(partial_terms, 'seq'), 'batch')]
  transfers between devices with their start and end apart: 1 -> 2, of which waited for: 1 -> 2; matrix products, arithmetic and copies ran while one was open for 0% -> 0% of each run, Pallas kernels for 0% -> 0%
where the time goes in v1:
time: 478 us
  waiting for transfers between devices  419 us (88%)
  between operations  15.8 us (3%)
  blocking collectives  15.2 us (3%)
  other arithmetic  12.2 us (3%)
  matrix products  10 us (2%)
  local copies, waits for them, and re-layouts  5.52 us (1%)
    psum x2, waiting for transfers between devices, local(): summed = lax.psum(lax.psum(partial_terms, 'seq'), 'batch')  419 us
    unnamed x1, blocking collectives  15.2 us
  transfers between devices with their start and end apart: 2, of which 2 were waited for; matrix products, arithmetic and copies ran while one was open for 0% of the time, Pallas kernels for 0%

profile of v1, /device:TPU:0, one launch (start us, length us, event | category | flops | bytes accessed | tf_op | source)
XLA Modules:
  0.0 477.9 jit_solution(5141042555328557608)
XLA Ops:
  7.2 0.0 copy-start
  7.2 0.0 all-reduce.4.cloned.1.call-start
  8.0 1.8 fusion.6
  9.9 0.5 slice.12
  10.4 1.2 dynamic-slice
  11.6 1.3 bitcast_dynamic-update-slice_fusion
  13.0 15.2 %all-reduce = f32[8]{0:T(128)S(1)} all-reduce(f32[8]{0:T(128)S(1)} %bitcast_dynamic-update-slice_fusion), channel_id=1, replica_groups=mesh['batch'=4,'seq'=8] {'seq'}, use_global_device_ids=true, to_apply=%add | all-reduce | flops 8 | bytes 64
  28.1 0.6 fusion.26
  28.7 0.0 copy-start.1
  28.7 4.3 fusion.1
  33.0 0.0 copy-done
  33.0 0.0 copy-done.1
  33.1 0.0 copy-start.4
  33.1 0.0 copy-start.5
  33.1 1.3 multiply_reduce_fusion.1
  34.5 0.7 multiply_add_fusion
  35.1 0.0 copy-start.3
  35.1 0.0 copy-done.4
  35.2 0.0 copy-done.5
  35.2 0.0 copy-start.2
  35.2 1.3 convolution_bitcast_fusion.1
  36.5 0.0 copy-done.3
  36.5 0.9 copy-done.2
  37.4 1.3 convolution_bitcast_fusion
  38.7 3.8 pad_maximum_fusion
  42.4 0.0 all-reduce.4.cloned.1.call-update
  42.4 0.0 all-reduce.6.cloned.1.call-start
  42.5 125.7 %all-reduce.4.cloned.1.call-done = f32[4096,512]{0,1:T(8,128)} async-done(((f32[4096,512]{0,1:T(8,128)}), f32[4096,512]{0,1:T(8,128)}) %all-reduce.4.cloned.1.call-update) | async-done | bytes 8388624 | tf_op jit(solution)/shard_map/psum | solution.py:67
  168.1 0.0 all-reduce.6.cloned.1.call-update
  168.2 293.4 %all-reduce.6.cloned.1.call-done = f32[4096,512]{0,1:T(8,128)} async-done(((f32[4096,512]{0,1:T(8,128)}), f32[4096,512]{0,1:T(8,128)}) %all-reduce.6.cloned.1.call-update) | async-done | bytes 8388624 | tf_op jit(solution)/shard_map/psum | solution.py:67
  461.6 6.1 %multiply_reduce_fusion = f32[]{:T(128)} fusion(f32[4096,512]{0,1:T(8,128)} %all-reduce.6.cloned.1.call-done), kind=kLoop, calls=%fused_computation.1 | loop fusion | flops 4194303 | bytes 8388612 | tf_op jit(solution)/shard_map/reduce_sum | solution.py:68
  468.5 1.0 dynamic-slice_multiply_fusion
  469.5 0.8 copy.12
  470.3 0.8 copy.11
  (3 shorter events, 0.0 us)
Async XLA Ops:
  7.2 25.9 %copy-start = (bf16[4096,256]{1,0:T(8,128)(2,1)S(1)}, bf16[4096,256]{1,0:T(8,128)(2,1)}, u32[]{:S(2)}) copy-start(bf16[4096,256]{1,0:T(8,128)(2,1)} %param.10) | copy-start | bytes 6291460
  7.2 161.0 %all-reduce.4.cloned.1.call-start = ((), (), s32[]{:S(2)}) async-start(), calls=%async_computation | async-start | bytes 16777216 | tf_op jit(solution)/shard_map/psum | solution.py:67
  28.7 4.3 copy-start.1
  33.1 2.1 copy-start.4
  33.1 2.1 copy-start.5
  35.1 1.4 copy-start.3
  35.2 2.2 copy-start.2
  42.4 419.2 %all-reduce.6.cloned.1.call-start = ((), (), s32[]{:S(2)}) async-start(), calls=%async_computation.1 | async-start | bytes 16777216 | tf_op jit(solution)/shard_map/psum | solution.py:67
Sparse Core Ops, SparseCore 0:
  42.6 125.5 all-reduce.3
  170.6 290.9 all-reduce.5
